TPU v7x, 32 devices: a whole 2x2x4 slice. The times are simulated.
32 devices in a mesh: dp: 16 (over z, y, core), tensor: 2 (over x).
Axes of the slice: x: 2, y: 2, z: 4, core: 2. Of those that a mesh axis runs over, the one named last changes fastest.
Arguments:
- tokens: bfloat16 [12288, 2048], P('dp'), may hold values from -6 to 6
- cotangent: bfloat16 [12288, 2048], P('dp'), may hold values from -8 to 8
- w_query: float32 [2048, 2048], P('dp', 'tensor'), may hold values from -0.125 to 0.125
- w_keyval: float32 [2048, 256], P('dp'), may hold values from -0.125 to 0.125
- w_out: float32 [2048, 2048], P('dp', 'tensor'), may hold values from -1 to 1
- w_up: float32 [2048, 8192], P('dp', 'tensor'), may hold values from -0.125 to 0.125
- w_down: float32 [2048, 8192], P('dp', 'tensor'), may hold values from -0.0625 to 0.0625
- norm1_gain: float32 [2048], P('dp'), may hold values from 0.25 to 1.75
- norm1_bias: float32 [2048], P('dp'), may hold values from -3 to 3
- norm2_gain: float32 [2048], P('dp'), may hold values from 0.25 to 1.75
- norm2_bias: float32 [2048], P('dp'), may hold values from -3 to 3
- route: int32 [12288], replicated, may hold values from 0 to 12287, as said below
- lengths: int32 [16, 4], P('dp'), may hold values from 1 to 512, 768 in all within a row
Outputs:
- output: bfloat16 [12288, 2048], P('dp')
- grad_tokens: bfloat16 [12288, 2048], P('dp')
- grad_w_query: float32 [2048, 2048], P('dp', 'tensor')
- grad_w_keyval: float32 [2048, 256], P('dp')
- grad_w_out: float32 [2048, 2048], P('dp', 'tensor')
- grad_w_up: float32 [2048, 8192], P('dp', 'tensor')
- grad_w_down: float32 [2048, 8192], P('dp', 'tensor')
- grad_norm1_gain: float32 [2048], P('dp')
- grad_norm1_bias: float32 [2048], P('dp')
- grad_norm2_gain: float32 [2048], P('dp')
- grad_norm2_bias: float32 [2048], P('dp')
Inputs may be any that keep to these rules, and one draw needn't show every extreme that they name: route is a permutation of the 12288 places; places g * 768 to (g + 1) * 768 - 1 belong to index g of dp, and the 768 tokens of each index of dp name exactly 48 places of every index of dp. Row g lists the lengths of the 4 sequences at index g of dp in order; they sum to 768, and the longest of each row is exactly 512.
All inputs are finite; a program needn't handle non-finite values.
Results may differ from a plain program's by a relative error of at most 0.012.
The roundings to bfloat16 on the way count: a program that leaves them out, or rounds other values in their place, can miss the bound.
Values may be sent and summed in bfloat16 or wider, within the bound.
A program may use at most 320 MiB of HBM per device.

v0:
```python
import jax
import jax.numpy as jnp
from jax import lax
from jax.sharding import PartitionSpec as P

norm_eps = 1e-05


def layer_norm(values, gain_vector, shift_vector):
    row_mean = jnp.mean(values, axis=-1, keepdims=True)
    centered = values - row_mean
    spread = jnp.mean(centered * centered, axis=-1, keepdims=True)
    return centered * lax.rsqrt(spread + norm_eps) * gain_vector + shift_vector


def gelu_tanh(values):
    return jax.nn.gelu(values, approximate=True)


def visible_pairs(lengths_row, row_count):
    boundaries = jnp.cumsum(lengths_row)
    places = jnp.arange(row_count, dtype=jnp.int32)
    segment = jnp.sum((places[:, None] >= boundaries[None, :]).astype(jnp.int32), axis=1)
    return jnp.logical_and(segment[:, None] == segment[None, :], places[None, :] <= places[:, None])


def right_product(first_op, second_op):
    return lax.dot_general(
        first_op, second_op, (((1,), (1,)), ((), ())), preferred_element_type=jnp.float32
    )


def left_product(first_op, second_op):
    return lax.dot_general(
        first_op, second_op, (((0,), (0,)), ((), ())), preferred_element_type=jnp.float32
    )


def column_term(first_op, second_op):
    return left_product(first_op, second_op)


def masked_scores(query_heads, key_rows, visible, score_scale):
    scores = (
        jnp.einsum("qhd,kd->hqk", query_heads, key_rows, preferred_element_type=jnp.float32)
        * score_scale
    )
    return jnp.where(visible, scores, -1e30)


def per_device(
    tokens,
    cotangent,
    w_query,
    w_keyval,
    w_out,
    w_up,
    w_down,
    norm1_gain,
    norm1_bias,
    norm2_gain,
    norm2_bias,
    route,
    lengths,
):
    row_count = tokens.shape[0]
    head_dim = w_keyval.shape[1] // 2
    heads_here = w_query.shape[1] // head_dim
    score_scale = head_dim ** (-0.5)
    group_index = lax.axis_index("dp")
    own_route = lax.dynamic_slice_in_dim(route, group_index * row_count, row_count)
    send_order = jnp.argsort(own_route, stable=True)
    inverse = jnp.argsort(route, stable=True)
    sources = lax.dynamic_slice_in_dim(inverse, group_index * row_count, row_count) // row_count
    recv_order = jnp.argsort(sources, stable=True)
    placing = jnp.argsort(recv_order, stable=True)
    arrived = (
        lax.all_to_all(tokens[send_order], "dp", split_axis=0, concat_axis=0, tiled=True),
        lax.all_to_all(cotangent[send_order], "dp", split_axis=0, concat_axis=0, tiled=True),
    )
    tokens_here = arrived[0][placing]
    grad_here = arrived[1][placing]
    fetched = (
        lax.all_gather(w_query.astype(jnp.bfloat16), "dp", axis=0, tiled=True),
        lax.all_gather(w_keyval.astype(jnp.bfloat16), "dp", axis=0, tiled=True),
        lax.all_gather(w_out.astype(jnp.bfloat16), "dp", axis=0, tiled=True),
        lax.all_gather(w_up.astype(jnp.bfloat16), "dp", axis=0, tiled=True),
        lax.all_gather(w_down.astype(jnp.bfloat16), "dp", axis=0, tiled=True),
        lax.all_gather(norm1_gain.astype(jnp.bfloat16), "dp", axis=0, tiled=True),
        lax.all_gather(norm1_bias.astype(jnp.bfloat16), "dp", axis=0, tiled=True),
        lax.all_gather(norm2_gain.astype(jnp.bfloat16), "dp", axis=0, tiled=True),
        lax.all_gather(norm2_bias.astype(jnp.bfloat16), "dp", axis=0, tiled=True),
    )
    full_query, full_keyval, full_out, full_up, full_down = (
        fetched[0],
        fetched[1],
        fetched[2],
        fetched[3],
        fetched[4],
    )
    first_gain = fetched[5].astype(jnp.float32)
    first_shift = fetched[6].astype(jnp.float32)
    second_gain = fetched[7].astype(jnp.float32)
    second_shift = fetched[8].astype(jnp.float32)
    resid_in = tokens_here.astype(jnp.float32)
    normed_one = layer_norm(resid_in, first_gain, first_shift).astype(jnp.bfloat16)
    queries = jnp.dot(normed_one, full_query, preferred_element_type=jnp.float32).astype(
        jnp.bfloat16
    )
    keyval = jnp.dot(normed_one, full_keyval, preferred_element_type=jnp.float32).astype(
        jnp.bfloat16
    )
    query_heads = queries.reshape(row_count, heads_here, head_dim)
    key_rows = keyval[:, :head_dim]
    value_rows = keyval[:, head_dim:]
    visible = visible_pairs(lengths[0], row_count)[None]
    masked = masked_scores(query_heads, key_rows, visible, score_scale)
    row_max = jnp.max(masked, axis=2, keepdims=True)
    weights_exp = jnp.exp(masked - row_max)
    row_total = jnp.sum(weights_exp, axis=2, keepdims=True)
    probs_first = (weights_exp / row_total).astype(jnp.bfloat16)
    log_total = row_max + jnp.log(row_total)
    context = jnp.einsum("hqk,kd->qhd", probs_first, value_rows, preferred_element_type=jnp.float32)
    context = context.reshape(row_count, heads_here * head_dim).astype(jnp.bfloat16)
    attn_output = lax.psum(right_product(context, full_out), "tensor")
    resid_mid = resid_in + attn_output
    normed_two = layer_norm(resid_mid, second_gain, second_shift).astype(jnp.bfloat16)
    hidden_pre = jnp.dot(normed_two, full_up, preferred_element_type=jnp.float32)
    active = gelu_tanh(hidden_pre).astype(jnp.bfloat16)
    mlp_output = lax.psum(right_product(active, full_down).astype(jnp.bfloat16), "tensor").astype(
        jnp.float32
    )
    result = (resid_mid + mlp_output).astype(jnp.bfloat16)
    refetched = (
        lax.all_gather(w_query.astype(jnp.bfloat16), "dp", axis=0, tiled=True),
        lax.all_gather(w_keyval.astype(jnp.bfloat16), "dp", axis=0, tiled=True),
        lax.all_gather(w_out.astype(jnp.bfloat16), "dp", axis=0, tiled=True),
        lax.all_gather(w_up.astype(jnp.bfloat16), "dp", axis=0, tiled=True),
        lax.all_gather(w_down.astype(jnp.bfloat16), "dp", axis=0, tiled=True),
    )
    back_query, back_keyval, back_out, back_up, back_down = (
        refetched[0],
        refetched[1],
        refetched[2],
        refetched[3],
        refetched[4],
    )
    grad_out = grad_here.astype(jnp.float32)
    grad_active = jnp.dot(grad_here, back_down, preferred_element_type=jnp.float32)
    gelu_back = jax.vjp(gelu_tanh, hidden_pre)[1]
    grad_up = gelu_back(grad_active)[0].astype(jnp.bfloat16)
    grad_norm_two = lax.psum(right_product(grad_up, back_up), "tensor")
    norm_two_back = jax.vjp(layer_norm, resid_mid, second_gain, second_shift)[1]
    grad_mid_norm, grad_gain_two, grad_shift_two = norm_two_back(grad_norm_two)
    grad_mid = grad_out + grad_mid_norm
    grad_mid_low = grad_mid.astype(jnp.bfloat16)
    grad_context = jnp.dot(grad_mid_low, back_out, preferred_element_type=jnp.float32).astype(
        jnp.bfloat16
    )
    grad_ctx_heads = grad_context.reshape(row_count, heads_here, head_dim)
    masked_again = masked_scores(query_heads, key_rows, visible, score_scale)
    probs_again = jnp.exp(masked_again - log_total)
    probs_low = probs_again.astype(jnp.bfloat16)
    grad_probs = jnp.einsum(
        "qhd,kd->hqk", grad_ctx_heads, value_rows, preferred_element_type=jnp.float32
    )
    row_delta = jnp.sum(grad_probs * probs_again, axis=2, keepdims=True)
    grad_scores = (probs_again * (grad_probs - row_delta)).astype(jnp.bfloat16)
    grad_query = (
        jnp.einsum("hqk,kd->qhd", grad_scores, key_rows, preferred_element_type=jnp.float32)
        * score_scale
    )
    grad_query = grad_query.reshape(row_count, heads_here * head_dim).astype(jnp.bfloat16)
    grad_keys = (
        jnp.einsum("hqk,qhd->kd", grad_scores, query_heads, preferred_element_type=jnp.float32)
        * score_scale
    )
    grad_values = jnp.einsum(
        "hqk,qhd->kd", probs_low, grad_ctx_heads, preferred_element_type=jnp.float32
    )
    grad_keyval_part = jnp.concatenate([grad_keys, grad_values], axis=1)
    grad_norm_query, grad_keyval = lax.psum(
        (right_product(grad_query, back_query), grad_keyval_part), "tensor"
    )
    grad_keyval_low = grad_keyval.astype(jnp.bfloat16)
    grad_norm_one = grad_norm_query + right_product(grad_keyval_low, back_keyval)
    norm_one_back = jax.vjp(layer_norm, resid_in, first_gain, first_shift)[1]
    grad_in_norm, grad_gain_one, grad_shift_one = norm_one_back(grad_norm_one)
    grad_resid = (grad_mid + grad_in_norm).astype(jnp.bfloat16)
    edge_one = w_query.shape[1]
    edge_two = edge_one + w_keyval.shape[1]
    up_cols = w_up.shape[1]
    summed = lax.psum_scatter(
        jnp.concatenate(
            [
                column_term(normed_one, grad_query),
                column_term(normed_one, grad_keyval_low),
                column_term(grad_mid_low, context),
                column_term(normed_two, grad_up),
                column_term(grad_here, active),
            ],
            axis=1,
        ),
        "dp",
        scatter_dimension=0,
        tiled=True,
    )
    edge_three = edge_two + w_out.shape[1]
    edge_four = edge_three + up_cols
    grad_wq = summed[:, :edge_one]
    grad_wkv = summed[:, edge_one:edge_two]
    grad_wo = summed[:, edge_two:edge_three]
    grad_wup = summed[:, edge_three:edge_four]
    grad_wdown = summed[:, edge_four:]
    norm_parts = (
        lax.psum_scatter(grad_gain_one, "dp", scatter_dimension=0, tiled=True),
        lax.psum_scatter(grad_shift_one, "dp", scatter_dimension=0, tiled=True),
        lax.psum_scatter(grad_gain_two, "dp", scatter_dimension=0, tiled=True),
        lax.psum_scatter(grad_shift_two, "dp", scatter_dimension=0, tiled=True),
    )
    returned = (
        lax.all_to_all(result[recv_order], "dp", split_axis=0, concat_axis=0, tiled=True),
        lax.all_to_all(grad_resid[recv_order], "dp", split_axis=0, concat_axis=0, tiled=True),
    )
    restore = jnp.argsort(send_order, stable=True)
    output = returned[0][restore]
    grad_tokens = returned[1][restore]
    return (
        output,
        grad_tokens,
        grad_wq,
        grad_wkv,
        grad_wo,
        grad_wup,
        grad_wdown,
        norm_parts[0],
        norm_parts[1],
        norm_parts[2],
        norm_parts[3],
    )


def solution(mesh):
    placed = (
        P("dp", None),
        P("dp", None),
        P("dp", "tensor"),
        P("dp", None),
        P("dp", "tensor"),
        P("dp", "tensor"),
        P("dp", "tensor"),
        P("dp"),
        P("dp"),
        P("dp"),
        P("dp"),
        P(),
        P("dp", None),
    )
    return jax.shard_map(
        per_device,
        mesh=mesh,
        in_specs=placed,
        out_specs=(
            P("dp", None),
            P("dp", None),
            P("dp", "tensor"),
            P("dp", None),
            P("dp", "tensor"),
            P("dp", "tensor"),
            P("dp", "tensor"),
            P("dp"),
            P("dp"),
            P("dp"),
            P("dp"),
        ),
        check_vma=False,
    )
```

profile of v0, /device:TPU:0, one launch (start us, length us, event | category | flops | bytes accessed | tf_op | source)
XLA Modules:
  0.0 1982.8 jit_solution(17851792786017311539)
XLA Ops:
  11.6 4.4 sort.76
  16.0 4.2 gather_fusion
  20.3 7.6 all-to-all-start
  29.9 69.7 %all-gather.1 = bf16[16,1,128]{2,1,0:T(2,128)(2,1)S(1)} all-gather(bf16[1,1,128]{2,1,0:T(2,128)(2,1)S(1)} %convert_bitcast_fusion.2), channel_id=1, replica_groups=mesh['dp'=16,'tensor'=2] {'dp'}, dimensions={0}, use_global_device_ids=true | all-gather | bytes 4352 | tf_op jit(solution)/shard_map/all_gather | solution.py:90
  99.6 48.6 %all-gather = bf16[16,1,128]{2,1,0:T(2,128)(2,1)S(1)} all-gather(bf16[1,1,128]{2,1,0:T(2,128)(2,1)S(1)} %convert_bitcast_fusion.3), channel_id=1, replica_groups=mesh['dp'=16,'tensor'=2] {'dp'}, dimensions={0}, use_global_device_ids=true | all-gather | bytes 4352 | tf_op jit(solution)/shard_map/all_gather | solution.py:89
  148.3 8.2 sort.77
  156.6 4.4 sort.78
  161.0 4.4 sort.79
  166.6 4.4 gather_fusion.1
  173.6 2.8 fusion.25
  177.6 2.9 fusion.23
  180.5 3.4 convolution_convert_fusion.3
  183.9 6.8 convolution_convert_fusion.2
  192.4 9.4 fusion.47
  201.8 8.9 fusion.3
  210.7 8.8 fusion.29
  219.6 8.2 fusion.48
  227.9 2.8 convert_element_type.142
  230.8 3.1 convert_element_type.140
  233.9 4.2 gather_fusion.4
  238.2 3.9 all-to-all-start.2
  242.1 67.0 %all-gather.3 = bf16[16,1,128]{2,1,0:T(2,128)(2,1)S(1)} all-gather(bf16[1,1,128]{2,1,0:T(2,128)(2,1)S(1)} %convert_bitcast_fusion), channel_id=1, replica_groups=mesh['dp'=16,'tensor'=2] {'dp'}, dimensions={0}, use_global_device_ids=true | all-gather | bytes 4352 | tf_op jit(solution)/shard_map/all_gather | solution.py:92
  309.2 32.8 %all-gather.2 = bf16[16,1,128]{2,1,0:T(2,128)(2,1)S(1)} all-gather(bf16[1,1,128]{2,1,0:T(2,128)(2,1)S(1)} %convert_bitcast_fusion.1), channel_id=1, replica_groups=mesh['dp'=16,'tensor'=2] {'dp'}, dimensions={0}, use_global_device_ids=true | all-gather | bytes 4352 | tf_op jit(solution)/shard_map/all_gather | solution.py:91
  342.0 4.7 gather_fusion.5
  346.7 31.9 %all-reduce.11.cloned.1.call-done = f32[768,2048]{1,0:T(8,128)} async-done(((f32[768,2048]{1,0:T(8,128)}), f32[768,2048]{1,0:T(8,128)}) %all-reduce.11.cloned.1.call-update) | async-done | bytes 6291472 | tf_op jit(solution)/shard_map/psum | solution.py:125
  378.5 4.4 fusion.44
  383.0 3.2 copy-done.5
  386.9 120.7 %all-gather.18.cloned.1.call-done = bf16[2048,4096]{1,0:T(8,128)(2,1)} async-done(((bf16[128,4096]{1,0:T(8,128)(2,1)}), bf16[2048,4096]{1,0:T(8,128)(2,1)}) %all-gather.18.cloned.1.call-update) | async-done | bytes 16777232 | tf_op jit(solution)/shard_map/all_gather | solution.py:88
  507.6 19.3 fusion.49
  526.9 107.9 %all-gather.16.cloned.1.call-done = bf16[2048,4096]{1,0:T(8,128)(2,1)} async-done(((bf16[128,4096]{1,0:T(8,128)(2,1)}), bf16[2048,4096]{1,0:T(8,128)(2,1)}) %all-gather.16.cloned.1.call-update) | async-done | bytes 16777232 | tf_op jit(solution)/shard_map/all_gather | solution.py:87
  634.8 30.8 %fusion.11 = (bf16[768,4096]{1,0:T(8,128)(2,1)}, f32[768,4096]{1,0:T(8,128)}) fusion(f32[768,4096]{1,0:T(8,128)} %fusion.49, bf16[2048,4096]{1,0:T(8,128)(2,1)} %all-gather.16.cloned.1.call-done, f32[768,2048]{1,0:T(8,128)} %copy-done.5, f32[2048]{0:T(1024)S(1)} %bitcast.116, f32[2048]{0:T(1024)S(1)} %bitcast.111, f32[768]{0:T(1024)S(1)} %fusion.39, ...), kind=kOutput, calls=%fused_computation.29 | convolution fusion | flops 12955680768 | bytes 54548480 | tf_op jit(solution)/shard_map/dot_general | solution.py:128
  665.7 20.5 %fusion.50 = f32[768,2048]{1,0:T(8,128)} fusion(bf16[768,4096]{1,0:T(8,128)(2,1)} %get-tuple-element.43, bf16[2048,4096]{1,0:T(8,128)(2,1)} %all-gather.16.cloned.1.call-done), kind=kOutput, calls=%fused_computation.118 | convolution fusion | flops 12884901888 | bytes 29360128 | tf_op jit(solution)/shard_map/dot_general | solution.py:28
  686.3 31.9 %convolution_convert_fusion = bf16[768,2048]{1,0:T(8,128)(2,1)} fusion(bf16[2048,4096]{1,0:T(8,128)(2,1)} %all-gather.18.cloned.1.call-done, f32[768,4096]{1,0:T(8,128)} %get-tuple-element.44), kind=kOutput, calls=%fused_computation.61 | convolution fusion | flops 12914786304 | bytes 32505856 | tf_op jit(solution)/shard_map/dot_general | solution.py:28
  718.3 119.5 %all-reduce.15.cloned.1.call-done = f32[768,2048]{1,0:T(8,128)} async-done(((f32[768,2048]{1,0:T(8,128)}), f32[768,2048]{1,0:T(8,128)}) %all-reduce.15.cloned.1.call-update) | async-done | bytes 6291472 | tf_op jit(solution)/shard_map/psum | solution.py:152
  837.8 6.8 multiply_reduce_fusion
  844.6 81.4 %all-reduce.13.cloned.1.call-done = bf16[768,2048]{1,0:T(8,128)(2,1)} async-done(((bf16[768,2048]{1,0:T(8,128)(2,1)}), bf16[768,2048]{1,0:T(8,128)(2,1)}) %all-reduce.13.cloned.1.call-update) | async-done | bytes 3145744 | tf_op jit(solution)/shard_map/psum | solution.py:130
  925.9 6.9 fusion.43
  938.1 4.5 convolution_convert_fusion.1
  945.2 8.5 fusion.31
  953.8 12.1 fusion
  965.9 12.9 fusion.2
  978.8 3.1 fusion.30
  981.9 2.7 multiply_convert_fusion.1
  985.5 22.9 %all-reduce.18 = bf16[768,256]{0,1:T(8,128)(2,1)S(1)} all-reduce(f32[768,256]{0,1:T(8,128)} %pad_maximum_fusion), channel_id=1, replica_groups=mesh['dp'=16,'tensor'=2] {'tensor'}, use_global_device_ids=true, to_apply=%region_20.21 | all-reduce | flops 196608 | bytes 1179648 | tf_op jit(solution)/shard_map/psum | solution.py:182
  1008.5 9.3 convolution_dynamic-update-slice_fusion.3
  1017.7 5.4 fusion.51
  1023.2 4.5 convolution_dynamic-update-slice_fusion.4
  1027.7 6.0 convolution_dynamic-update-slice_fusion.2
  1033.7 23.6 %convolution_dynamic-update-slice_fusion.1 = f32[2048,10496]{1,0:T(8,128)} fusion(f32[2048,10496]{1,0:T(8,128)} %convolution_dynamic-update-slice_fusion.2, bf16[768,4096]{1,0:T(8,128)(2,1)} %get-tuple-element.43, f32[768,2048]{1,0:T(8,128)} %copy-done.5, f32[2048]{0:T(1024)S(1)} %bitcast.117, f32[2048]{0:T(1024)S(1)} %bitcast.114, f32[768]{0:T(1024)S(1)} %fusion.39, ...), kind=kOutput, calls=%fused_computation.9 | convolution fusion | flops 12892766208 | bytes 46159872 | tf_op jit(solution)/shard_map/dot_general | solution.py:34
  1057.3 25.4 %convolution_dynamic-update-slice_fusion = f32[2048,10496]{1,0:T(8,128)} fusion(f32[2048,10496]{1,0:T(8,128)} %convolution_dynamic-update-slice_fusion.1, bf16[768,2048]{1,0:T(8,128)(2,1)} %gather_fusion.5, f32[768,4096]{1,0:T(8,128)} %get-tuple-element.44), kind=kOutput, calls=%fused_computation.8 | convolution fusion | flops 12913213440 | bytes 49283072 | tf_op jit(solution)/shard_map/dot_general | solution.py:34
  1084.0 4.3 gather_fusion.2
  1088.3 5.9 all-to-all-start.1
  1094.2 83.2 %all-reduce.17.cloned.1.call-done = f32[768,2048]{1,0:T(8,128)} async-done(((f32[768,2048]{1,0:T(8,128)}), f32[768,2048]{1,0:T(8,128)}) %all-reduce.17.cloned.1.call-update) | async-done | bytes 6291472 | tf_op jit(solution)/shard_map/psum | solution.py:182
  1177.3 6.1 fusion.42
  1183.5 3.0 fusion.24
  1186.5 6.3 add_convert_fusion
  1192.8 10.1 gather_fusion.6
  1203.0 6.2 all-to-all-start.3
  1209.2 4.4 sort.80
  1214.9 4.2 gather_fusion.3
  1219.1 100.9 %all-reduce.4 = (f32[2048]{0:T(1024)S(1)}, f32[2048]{0:T(1024)S(1)}, f32[2048]{0:T(1024)S(1)}, f32[2048]{0:T(1024)S(1)}) all-reduce(f32[2048]{0:T(1024)S(1)} %get-tuple-element.23, f32[2048]{0:T(1024)S(1)} %copy-done.36, f32[2048]{0:T(1024)S(1)} %copy-done.37, f32[2048]{0:T(1024)S(1)} %copy-done.38), channel_id=3, replica_groups=mesh['dp'=16,'tensor'=2] {'dp'}, use_global_device_ids=true, to_apply=%region_25.26.clone | all-reduce | flops 8192 | bytes 65536
  1322.3 9.6 gather_fusion.7
  1331.9 635.1 %reduce-scatter.2.cloned.1.call-done = f32[128,10496]{1,0:T(8,128)} async-done(((f32[2048,10496]{1,0:T(8,128)}), f32[128,10496]{1,0:T(8,128)}) %reduce-scatter.2.cloned.1.call-update) | async-done | bytes 5373968 | tf_op jit(solution)/shard_map/reduce_scatter | solution.py:193
  1970.8 4.7 fusion.45
  (187 shorter events, 31.5 us)
Async XLA Ops:
  7.2 8.8 copy-start
  7.2 173.3 %all-gather.10.cloned.1.call-start = ((), (), s32[]{:S(2)}) async-start(), calls=%async_computation.5 | async-start | bytes 1114112 | tf_op jit(solution)/shard_map/all_gather | solution.py:85
  9.0 174.9 %all-gather.12.cloned.1.call-start = ((), (), s32[]{:S(2)}) async-start(), calls=%async_computation.6 | async-start | bytes 4456448 | tf_op jit(solution)/shard_map/all_gather | solution.py:84
  16.0 4.3 copy-start.39
  20.2 9.5 copy-start.47
  20.2 9.5 copy-start.48
  20.2 9.5 copy-start.49
  20.2 128.1 %copy-start.29 = (s32[12288]{0:T(1024)S(1)}, s32[12288]{0:T(1024)}, u32[]{:S(2)}) copy-start(s32[12288]{0:T(1024)} %param.24) | copy-start | bytes 147460
  20.3 146.4 %all-to-all-start = ((bf16[16,48,2048]{2,1,0:T(8,128)(2,1)}), bf16[16,48,2048]{2,1,0:T(8,128)(2,1)S(1)}, u32[]{:S(2)}, u32[]{:S(2)}) async-start(bf16[16,48,2048]{2,1,0:T(8,128)(2,1)} %bitcast.99), calls=%async_computation | async-start | bytes 6291456 | tf_op jit(solution)/shard_map/all_to_all | solution.py:78
  27.8 191.8 %all-gather.14.cloned.1.call-start = ((), (), s32[]{:S(2)}) async-start(), calls=%async_computation.7 | async-start | bytes 4456448 | tf_op jit(solution)/shard_map/all_gather | solution.py:86
  29.7 348.9 %all-reduce.11.cloned.1.call-start = ((), (), s32[]{:S(2)}) async-start(), calls=%async_computation.8 | async-start | bytes 12582912 | tf_op jit(solution)/shard_map/psum | solution.py:125
  148.3 28.8 %copy-start.21 = (f32[16,1,128]{2,1,0:T(1,128)}, f32[16,1,128]{2,1,0:T(1,128)S(1)}, u32[]{:S(2)}) copy-start(f32[16,1,128]{2,1,0:T(1,128)S(1)} %convert_element_type.157) | copy-start | bytes 24580
  161.0 10.1 copy-start.41
  171.1 6.6 copy-start.2
  173.6 3.5 copy-start.23
  180.5 3.4 copy-start.10
  183.9 26.8 %copy-start.17 = (bf16[768,256]{1,0:T(8,128)(2,1)}, bf16[768,256]{1,0:T(8,128)(2,1)S(1)}, u32[]{:S(2)}) copy-start(bf16[768,256]{1,0:T(8,128)(2,1)S(1)} %convolution_convert_fusion.3) | copy-start | bytes 1179652
  192.4 9.4 copy-start.12
  201.8 8.9 copy-start.19
  210.7 8.9 copy-start.25
  219.6 8.3 copy-start.52
  227.8 6.1 copy-start.4
  227.9 279.7 %all-gather.18.cloned.1.call-start = ((), (), s32[]{:S(2)}) async-start(), calls=%async_computation.10 | async-start | bytes 17825792 | tf_op jit(solution)/shard_map/all_gather | solution.py:88
  230.8 404.0 %all-gather.16.cloned.1.call-start = ((), (), s32[]{:S(2)}) async-start(), calls=%async_computation.9 | async-start | bytes 17825792 | tf_op jit(solution)/shard_map/all_gather | solution.py:87
  238.2 3.9 copy-start.50
  238.2 71.0 %copy-start.51 = (f32[128]{0:T(128)S(1)}, f32[128]{0:T(128)}, u32[]{:S(2)}) copy-start(f32[128]{0:T(128)} %param.22) | copy-start | bytes 1540
  238.2 103.8 %all-to-all-start.2 = ((bf16[16,48,2048]{2,1,0:T(8,128)(2,1)}), bf16[16,48,2048]{2,1,0:T(8,128)(2,1)S(1)}, u32[]{:S(2)}, u32[]{:S(2)}) async-start(bf16[16,48,2048]{2,1,0:T(8,128)(2,1)} %bitcast.102), calls=%async_computation.2 | async-start | bytes 6291456 | tf_op jit(solution)/shard_map/all_to_all | solution.py:79
  242.1 595.7 %all-reduce.15.cloned.1.call-start = ((), (), s32[]{:S(2)}) async-start(), calls=%async_computation.12 | async-start | bytes 12582912 | tf_op jit(solution)/shard_map/psum | solution.py:152
  309.1 325.7 %copy-start.43 = (f32[16,1,128]{2,1,0:T(1,128)}, f32[16,1,128]{2,1,0:T(1,128)S(1)}, u32[]{:S(2)}) copy-start(f32[16,1,128]{2,1,0:T(1,128)S(1)} %convert_element_type.160) | copy-start | bytes 24580
  382.9 3.2 copy-start.5
  382.9 124.7 %copy-start.7 = (bf16[768,2048]{1,0:T(8,128)(2,1)S(1)}, bf16[768,2048]{1,0:T(8,128)(2,1)}, u32[]{:S(2)}) copy-start(bf16[768,2048]{1,0:T(8,128)(2,1)} %gather_fusion.5) | copy-start | bytes 9437188
  686.2 239.7 %all-reduce.13.cloned.1.call-start = ((), (), s32[]{:S(2)}) async-start(), calls=%async_computation.11 | async-start | bytes 6291456 | tf_op jit(solution)/shard_map/psum | solution.py:130
  686.3 32.0 %copy-start.20 = (f32[8,768]{1,0:T(8,128)S(1)}, f32[8,768]{1,0:T(8,128)}, u32[]{:S(2)}) copy-start(f32[8,768]{1,0:T(8,128)} %copy-done.19) | copy-start | bytes 73732
  686.3 32.0 %copy-start.26 = (f32[8,768]{1,0:T(8,128)S(1)}, f32[8,768]{1,0:T(8,128)}, u32[]{:S(2)}) copy-start(f32[8,768]{1,0:T(8,128)} %copy-done.25) | copy-start | bytes 73732
  718.2 459.1 %all-reduce.17.cloned.1.call-start = ((), (), s32[]{:S(2)}) async-start(), calls=%async_computation.13 | async-start | bytes 12582912 | tf_op jit(solution)/shard_map/psum | solution.py:182
  925.9 6.9 copy-start.8
  932.8 3.2 copy-start.6
  932.8 3.2 copy-start.30
  932.8 5.3 copy-start.46
  945.2 8.5 copy-start.11
  945.2 8.5 copy-start.18
  965.9 12.9 copy-start.13
  1008.4 9.3 copy-start.16
  1008.5 9.3 copy-start.45
  1023.1 943.8 %reduce-scatter.2.cloned.1.call-start = ((), (), s32[]{:S(2)}) async-start(), calls=%async_computation.14 | async-start | bytes 91357184 | tf_op jit(solution)/shard_map/reduce_scatter | solution.py:193
  1023.2 4.5 copy-start.15
  1023.2 4.5 copy-start.53
  1027.7 6.0 copy-start.44
  1088.3 89.1 %copy-start.22 = (f32[16,1,128]{2,1,0:T(1,128)S(1)}, f32[16,1,128]{2,1,0:T(1,128)}, u32[]{:S(2)}) copy-start(f32[16,1,128]{2,1,0:T(1,128)} %copy-done.21) | copy-start | bytes 24580
  1088.3 89.1 %copy-start.24 = (f32[768]{0:T(1024)S(1)}, f32[768]{0:T(1024)}, u32[]{:S(2)}) copy-start(f32[768]{0:T(1024)} %copy-done.23) | copy-start | bytes 9220
  1088.3 114.7 %all-to-all-start.1 = ((bf16[16,48,2048]{2,1,0:T(8,128)(2,1)}), bf16[16,48,2048]{2,1,0:T(8,128)(2,1)S(1)}, u32[]{:S(2)}, u32[]{:S(2)}) async-start(bf16[16,48,2048]{2,1,0:T(8,128)(2,1)} %bitcast.101), calls=%async_computation.1 | async-start | bytes 6291456 | tf_op jit(solution)/shard_map/all_to_all | solution.py:222
  1094.1 89.3 %copy-start.28 = (f32[768]{0:T(1024)S(1)}, f32[768]{0:T(1024)}, u32[]{:S(2)}) copy-start(f32[768]{0:T(1024)} %copy-done.27) | copy-start | bytes 9220
  1177.3 6.1 copy-start.33
  1177.3 6.2 copy-start.3
  1183.5 3.0 copy-start.9
  1183.5 3.0 copy-start.31
  1186.5 6.3 copy-start.35
  1203.0 6.2 copy-start.40
  1203.0 10.6 copy-start.54
  1203.0 119.4 %all-to-all-start.3 = ((bf16[16,48,2048]{2,1,0:T(8,128)(2,1)}), bf16[16,48,2048]{2,1,0:T(8,128)(2,1)}, u32[]{:S(2)}, u32[]{:S(2)}) async-start(bf16[16,48,2048]{2,1,0:T(8,128)(2,1)} %bitcast.100), calls=%async_computation.3 | async-start | bytes 6291456 | tf_op jit(solution)/shard_map/all_to_all | solution.py:223
  1214.9 4.3 copy-start.36
  1214.9 4.3 copy-start.37
  1214.9 4.3 copy-start.38
  1322.3 653.2 %copy-start.1 = (bf16[768,2048]{1,0:T(8,128)(2,1)S(1)}, bf16[768,2048]{1,0:T(8,128)(2,1)}, u32[]{:S(2)}) copy-start(bf16[768,2048]{1,0:T(8,128)(2,1)} %param.13) | copy-start | bytes 9437188
  (5 other events, 4.1 us)
Sparse Core Ops, SparseCore 0:
  10.7 62.2 all-gather.9
  75.7 56.6 all-gather.11
  134.6 50.0 all-gather.13
  228.0 150.5 all-reduce.10
  381.1 126.4 all-gather.17
  510.2 124.5 all-gather.15
  686.3 151.4 all-reduce.14
  840.1 85.8 all-reduce.12
  1023.3 154.0 all-reduce.16
  1181.4 785.5 reduce-scatter.1
where the time goes:
time: 1990 us; the launch traced here: 1980 us
  waiting for transfers between devices  1180 us (59%)
  blocking collectives  342 us (17%)
  matrix products  250 us (13%)
  other arithmetic  98.3 us (5%)
  local copies, waits for them, and re-layouts  72.6 us (4%)
  starting transfers between devices  23.9 us (1%)
    reduce_scatter x1, waiting for transfers between devices, per_device(): lax.psum_scatter(jnp.concatenate([column_term(normed_one, grad_query), co...  635 us
    all_gather x1, waiting for transfers between devices, per_device(): lax.all_gather(w_down.astype(jnp.bfloat16), 'dp', axis=0, tiled=True)  121 us
    psum x1, waiting for transfers between devices, per_device(): grad_norm_two = lax.psum(right_product(grad_up, back_up), 'tensor')  120 us
    all_gather x1, waiting for transfers between devices, per_device(): lax.all_gather(w_up.astype(jnp.bfloat16), 'dp', axis=0, tiled=True)  108 us
    unnamed x1, blocking collectives  101 us
    psum x1, waiting for transfers between devices, per_device(): lax.psum((right_product(grad_query, back_query), grad_keyval_part), 'tens...  83.2 us
    psum x1, waiting for transfers between devices, per_device(): lax.psum(right_product(active, full_down).astype(jnp.bfloat16), 'tensor')  81.4 us
    dot_general x5, matrix products, right_product(): lax.dot_general(first_op, second_op, (((1,), (1,)), ((), ())), preferred_...  72.1 us
  transfers between devices with their start and end apart: 14, of which 7 were waited for; matrix products, arithmetic and copies ran while one was open for 14% of the time, Pallas kernels for 0%

commit v1 on v0

--- a/solution.py
+++ b/solution.py
@@ -127,9 +127,9 @@
     normed_two = layer_norm(resid_mid, second_gain, second_shift).astype(jnp.bfloat16)
     hidden_pre = jnp.dot(normed_two, full_up, preferred_element_type=jnp.float32)
     active = gelu_tanh(hidden_pre).astype(jnp.bfloat16)
-    mlp_output = lax.psum(right_product(active, full_down).astype(jnp.bfloat16), "tensor").astype(
-        jnp.float32
-    )
+    mlp_output = jnp.sum(
+        lax.all_gather(right_product(active, full_down).astype(jnp.bfloat16), "tensor"), axis=0
+    ).astype(jnp.float32)
     result = (resid_mid + mlp_output).astype(jnp.bfloat16)
     refetched = (
         lax.all_gather(w_query.astype(jnp.bfloat16), "dp", axis=0, tiled=True),

time: 1990 us -> 1990 us (level)
    psum x1 -> x0, waiting for transfers between devices: 81.4 us -> none  [per_device(): lax.psum(right_product(active, full_down).astype(jnp.bfloat16), 'tensor')]
    all_gather x0 -> x1, waiting for transfers between devices: none -> 75.4 us  [per_device(): lax.all_gather(right_product(active, full_down).astype(jnp.bfloat16), 'te...]
where the time goes in v1:
time: 1990 us; the launch traced here: 1980 us
  waiting for transfers between devices  1170 us (59%)
  blocking collectives  342 us (17%)
  matrix products  251 us (13%)
  other arithmetic  105 us (5%)
  local copies, waits for them, and re-layouts  72.5 us (4%)
  starting transfers between devices  23.8 us (1%)
    reduce_scatter x1, waiting for transfers between devices, per_device(): lax.psum_scatter(jnp.concatenate([column_term(normed_one, grad_query), co...  635 us
    all_gather x1, waiting for transfers between devices, per_device(): lax.all_gather(w_down.astype(jnp.bfloat16), 'dp', axis=0, tiled=True)  121 us
    psum x1, waiting for transfers between devices, per_device(): grad_norm_two = lax.psum(right_product(grad_up, back_up), 'tensor')  120 us
    all_gather x1, waiting for transfers between devices, per_device(): lax.all_gather(w_up.astype(jnp.bfloat16), 'dp', axis=0, tiled=True)  108 us
    unnamed x1, blocking collectives  101 us
    psum x1, waiting for transfers between devices, per_device(): lax.psum((right_product(grad_query, back_query), grad_keyval_part), 'tens...  83.1 us
    all_gather x1, waiting for transfers between devices, per_device(): lax.all_gather(right_product(active, full_down).astype(jnp.bfloat16), 'te...  75.4 us
    dot_general x5, matrix products, right_product(): lax.dot_general(first_op, second_op, (((1,), (1,)), ((), ())), preferred_...  72.4 us
  transfers between devices with their start and end apart: 14, of which 7 were waited for; matrix products, arithmetic and copies ran while one was open for 14% of the time, Pallas kernels for 0%

profile of v1, /device:TPU:0, one launch (start us, length us, event | category | flops | bytes accessed | tf_op | source)
XLA Modules:
  0.0 1983.5 jit_solution(15407352050042404907)
XLA Ops:
  11.6 4.4 sort.76
  16.0 4.2 gather_fusion
  20.3 7.6 all-to-all-start
  30.0 69.7 %all-gather.2 = bf16[16,1,128]{2,1,0:T(2,128)(2,1)S(1)} all-gather(bf16[1,1,128]{2,1,0:T(2,128)(2,1)S(1)} %convert_bitcast_fusion.2), channel_id=1, replica_groups=mesh['dp'=16,'tensor'=2] {'dp'}, dimensions={0}, use_global_device_ids=true | all-gather | bytes 4352 | tf_op jit(solution)/shard_map/all_gather | solution.py:90
  99.6 48.6 %all-gather.1 = bf16[16,1,128]{2,1,0:T(2,128)(2,1)S(1)} all-gather(bf16[1,1,128]{2,1,0:T(2,128)(2,1)S(1)} %convert_bitcast_fusion.3), channel_id=1, replica_groups=mesh['dp'=16,'tensor'=2] {'dp'}, dimensions={0}, use_global_device_ids=true | all-gather | bytes 4352 | tf_op jit(solution)/shard_map/all_gather | solution.py:89
  148.3 8.2 sort.77
  156.6 4.4 sort.78
  161.0 4.4 sort.79
  166.6 4.7 gather_fusion.1
  173.8 2.8 fusion.25
  177.9 2.9 fusion.23
  180.7 3.4 convolution_convert_fusion.3
  184.2 6.8 convolution_convert_fusion.2
  192.7 9.4 fusion.47
  202.1 8.9 fusion.3
  211.0 8.8 fusion.29
  219.8 8.2 fusion.48
  228.1 2.8 convert_element_type.144
  231.1 3.1 convert_element_type.142
  234.2 4.2 gather_fusion.4
  238.4 3.9 all-to-all-start.2
  242.4 67.0 %all-gather.4 = bf16[16,1,128]{2,1,0:T(2,128)(2,1)S(1)} all-gather(bf16[1,1,128]{2,1,0:T(2,128)(2,1)S(1)} %convert_bitcast_fusion), channel_id=1, replica_groups=mesh['dp'=16,'tensor'=2] {'dp'}, dimensions={0}, use_global_device_ids=true | all-gather | bytes 4352 | tf_op jit(solution)/shard_map/all_gather | solution.py:92
  309.4 32.8 %all-gather.3 = bf16[16,1,128]{2,1,0:T(2,128)(2,1)S(1)} all-gather(bf16[1,1,128]{2,1,0:T(2,128)(2,1)S(1)} %convert_bitcast_fusion.1), channel_id=1, replica_groups=mesh['dp'=16,'tensor'=2] {'dp'}, dimensions={0}, use_global_device_ids=true | all-gather | bytes 4352 | tf_op jit(solution)/shard_map/all_gather | solution.py:91
  342.2 4.4 gather_fusion.5
  346.7 32.1 %all-reduce.10.cloned.1.call-done = f32[768,2048]{1,0:T(8,128)} async-done(((f32[768,2048]{1,0:T(8,128)}), f32[768,2048]{1,0:T(8,128)}) %all-reduce.10.cloned.1.call-update) | async-done | bytes 6291472 | tf_op jit(solution)/shard_map/psum | solution.py:125
  378.8 4.4 fusion.44
  383.2 3.2 copy-done.5
  387.1 120.7 %all-gather.20.cloned.1.call-done = bf16[2048,4096]{1,0:T(8,128)(2,1)} async-done(((bf16[128,4096]{1,0:T(8,128)(2,1)}), bf16[2048,4096]{1,0:T(8,128)(2,1)}) %all-gather.20.cloned.1.call-update) | async-done | bytes 16777232 | tf_op jit(solution)/shard_map/all_gather | solution.py:88
  507.8 19.3 fusion.49
  527.2 107.9 %all-gather.18.cloned.1.call-done = bf16[2048,4096]{1,0:T(8,128)(2,1)} async-done(((bf16[128,4096]{1,0:T(8,128)(2,1)}), bf16[2048,4096]{1,0:T(8,128)(2,1)}) %all-gather.18.cloned.1.call-update) | async-done | bytes 16777232 | tf_op jit(solution)/shard_map/all_gather | solution.py:87
  635.0 30.9 %fusion.11 = (bf16[768,4096]{1,0:T(8,128)(2,1)}, f32[768,4096]{1,0:T(8,128)}) fusion(f32[768,4096]{1,0:T(8,128)} %fusion.49, bf16[2048,4096]{1,0:T(8,128)(2,1)} %all-gather.18.cloned.1.call-done, f32[768,2048]{1,0:T(8,128)} %copy-done.5, f32[2048]{0:T(1024)S(1)} %bitcast.118, f32[2048]{0:T(1024)S(1)} %bitcast.113, f32[768]{0:T(1024)S(1)} %fusion.39, ...), kind=kOutput, calls=%fused_computation.29 | convolution fusion | flops 12955680768 | bytes 54548480 | tf_op jit(solution)/shard_map/dot_general | solution.py:128
  665.9 20.8 %fusion.50 = f32[768,2048]{1,0:T(8,128)} fusion(bf16[768,4096]{1,0:T(8,128)(2,1)} %get-tuple-element.43, bf16[2048,4096]{1,0:T(8,128)(2,1)} %all-gather.18.cloned.1.call-done), kind=kOutput, calls=%fused_computation.118 | convolution fusion | flops 12884901888 | bytes 29360128 | tf_op jit(solution)/shard_map/dot_general | solution.py:28
  686.8 31.8 %convolution_convert_fusion = bf16[768,2048]{1,0:T(8,128)(2,1)} fusion(bf16[2048,4096]{1,0:T(8,128)(2,1)} %all-gather.20.cloned.1.call-done, f32[768,4096]{1,0:T(8,128)} %get-tuple-element.44), kind=kOutput, calls=%fused_computation.61 | convolution fusion | flops 12914786304 | bytes 32505856 | tf_op jit(solution)/shard_map/dot_general | solution.py:28
  718.8 119.5 %all-reduce.12.cloned.1.call-done = f32[768,2048]{1,0:T(8,128)} async-done(((f32[768,2048]{1,0:T(8,128)}), f32[768,2048]{1,0:T(8,128)}) %all-reduce.12.cloned.1.call-update) | async-done | bytes 6291472 | tf_op jit(solution)/shard_map/psum | solution.py:152
  838.3 6.5 multiply_reduce_fusion
  844.9 75.4 %all-gather.22.cloned.1.call-done = bf16[1536,2048]{1,0:T(8,128)(2,1)} async-done(((bf16[768,2048]{1,0:T(8,128)(2,1)}), bf16[1536,2048]{1,0:T(8,128)(2,1)}) %all-gather.22.cloned.1.call-update) | async-done | bytes 6291472 | tf_op jit(solution)/shard_map/all_gather | solution.py:131
  920.2 6.8 reduce_sum.155
  927.1 6.9 fusion.43
  939.3 4.5 convolution_convert_fusion.1
  946.4 8.5 fusion.31
  954.9 12.1 fusion
  967.0 13.1 fusion.2
  980.2 3.1 fusion.30
  986.9 22.8 %all-reduce.15 = bf16[768,256]{0,1:T(8,128)(2,1)S(1)} all-reduce(f32[768,256]{0,1:T(8,128)} %pad_maximum_fusion), channel_id=1, replica_groups=mesh['dp'=16,'tensor'=2] {'tensor'}, use_global_device_ids=true, to_apply=%region_20.21 | all-reduce | flops 196608 | bytes 1179648 | tf_op jit(solution)/shard_map/psum | solution.py:182
  1009.7 9.3 convolution_dynamic-update-slice_fusion.3
  1019.0 5.4 fusion.51
  1024.4 4.5 convolution_dynamic-update-slice_fusion.4
  1029.0 6.2 convolution_dynamic-update-slice_fusion.2
  1035.1 23.6 %convolution_dynamic-update-slice_fusion.1 = f32[2048,10496]{1,0:T(8,128)} fusion(f32[2048,10496]{1,0:T(8,128)} %convolution_dynamic-update-slice_fusion.2, bf16[768,4096]{1,0:T(8,128)(2,1)} %get-tuple-element.43, f32[768,2048]{1,0:T(8,128)} %copy-done.5, f32[2048]{0:T(1024)S(1)} %bitcast.119, f32[2048]{0:T(1024)S(1)} %bitcast.116, f32[768]{0:T(1024)S(1)} %fusion.39, ...), kind=kOutput, calls=%fused_computation.9 | convolution fusion | flops 12892766208 | bytes 46159872 | tf_op jit(solution)/shard_map/dot_general | solution.py:34
  1058.7 25.3 %convolution_dynamic-update-slice_fusion = f32[2048,10496]{1,0:T(8,128)} fusion(f32[2048,10496]{1,0:T(8,128)} %convolution_dynamic-update-slice_fusion.1, bf16[768,2048]{1,0:T(8,128)(2,1)} %gather_fusion.5, f32[768,4096]{1,0:T(8,128)} %get-tuple-element.44), kind=kOutput, calls=%fused_computation.8 | convolution fusion | flops 12913213440 | bytes 49283072 | tf_op jit(solution)/shard_map/dot_general | solution.py:34
  1085.3 4.3 gather_fusion.2
  1089.6 5.8 all-to-all-start.1
  1095.4 83.1 %all-reduce.14.cloned.1.call-done = f32[768,2048]{1,0:T(8,128)} async-done(((f32[768,2048]{1,0:T(8,128)}), f32[768,2048]{1,0:T(8,128)}) %all-reduce.14.cloned.1.call-update) | async-done | bytes 6291472 | tf_op jit(solution)/shard_map/psum | solution.py:182
  1178.5 6.1 fusion.42
  1184.6 3.0 fusion.24
  1187.7 6.3 add_convert_fusion
  1194.0 10.1 gather_fusion.6
  1204.1 6.2 all-to-all-start.3
  1210.3 4.4 sort.80
  1216.0 4.2 gather_fusion.3
  1220.2 100.9 %all-reduce.4 = (f32[2048]{0:T(1024)S(1)}, f32[2048]{0:T(1024)S(1)}, f32[2048]{0:T(1024)S(1)}, f32[2048]{0:T(1024)S(1)}) all-reduce(f32[2048]{0:T(1024)S(1)} %get-tuple-element.23, f32[2048]{0:T(1024)S(1)} %copy-done.36, f32[2048]{0:T(1024)S(1)} %copy-done.37, f32[2048]{0:T(1024)S(1)} %copy-done.38), channel_id=4, replica_groups=mesh['dp'=16,'tensor'=2] {'dp'}, use_global_device_ids=true, to_apply=%region_25.26.clone | all-reduce | flops 8192 | bytes 65536
  1323.4 9.6 gather_fusion.7
  1333.0 634.9 %reduce-scatter.2.cloned.1.call-done = f32[128,10496]{1,0:T(8,128)} async-done(((f32[2048,10496]{1,0:T(8,128)}), f32[128,10496]{1,0:T(8,128)}) %reduce-scatter.2.cloned.1.call-update) | async-done | bytes 5373968 | tf_op jit(solution)/shard_map/reduce_scatter | solution.py:193
  1971.8 4.7 fusion.45
  (188 shorter events, 34.2 us)
Async XLA Ops:
  7.2 8.8 copy-start
  7.2 173.6 %all-gather.12.cloned.1.call-start = ((), (), s32[]{:S(2)}) async-start(), calls=%async_computation.5 | async-start | bytes 1114112 | tf_op jit(solution)/shard_map/all_gather | solution.py:85
  9.0 175.2 %all-gather.14.cloned.1.call-start = ((), (), s32[]{:S(2)}) async-start(), calls=%async_computation.6 | async-start | bytes 4456448 | tf_op jit(solution)/shard_map/all_gather | solution.py:84
  16.0 4.3 copy-start.39
  20.2 9.5 copy-start.47
  20.2 9.5 copy-start.48
  20.2 9.5 copy-start.49
  20.2 128.1 %copy-start.29 = (s32[12288]{0:T(1024)S(1)}, s32[12288]{0:T(1024)}, u32[]{:S(2)}) copy-start(s32[12288]{0:T(1024)} %param.24) | copy-start | bytes 147460
  20.3 146.4 %all-to-all-start = ((bf16[16,48,2048]{2,1,0:T(8,128)(2,1)}), bf16[16,48,2048]{2,1,0:T(8,128)(2,1)S(1)}, u32[]{:S(2)}, u32[]{:S(2)}) async-start(bf16[16,48,2048]{2,1,0:T(8,128)(2,1)} %bitcast.100), calls=%async_computation | async-start | bytes 6291456 | tf_op jit(solution)/shard_map/all_to_all | solution.py:78
  27.8 192.0 %all-gather.16.cloned.1.call-start = ((), (), s32[]{:S(2)}) async-start(), calls=%async_computation.7 | async-start | bytes 4456448 | tf_op jit(solution)/shard_map/all_gather | solution.py:86
  29.7 349.1 %all-reduce.10.cloned.1.call-start = ((), (), s32[]{:S(2)}) async-start(), calls=%async_computation.8 | async-start | bytes 12582912 | tf_op jit(solution)/shard_map/psum | solution.py:125
  148.3 29.0 %copy-start.21 = (f32[16,1,128]{2,1,0:T(1,128)}, f32[16,1,128]{2,1,0:T(1,128)S(1)}, u32[]{:S(2)}) copy-start(f32[16,1,128]{2,1,0:T(1,128)S(1)} %convert_element_type.159) | copy-start | bytes 24580
  161.0 10.3 copy-start.41
  171.3 6.6 copy-start.2
  173.8 3.5 copy-start.23
  180.7 3.5 copy-start.10
  184.2 26.8 %copy-start.17 = (bf16[768,256]{1,0:T(8,128)(2,1)}, bf16[768,256]{1,0:T(8,128)(2,1)S(1)}, u32[]{:S(2)}) copy-start(bf16[768,256]{1,0:T(8,128)(2,1)S(1)} %convolution_convert_fusion.3) | copy-start | bytes 1179652
  192.7 9.4 copy-start.12
  202.1 8.9 copy-start.19
  211.0 8.8 copy-start.25
  219.8 8.3 copy-start.52
  228.1 6.1 copy-start.4
  228.1 279.7 %all-gather.20.cloned.1.call-start = ((), (), s32[]{:S(2)}) async-start(), calls=%async_computation.10 | async-start | bytes 17825792 | tf_op jit(solution)/shard_map/all_gather | solution.py:88
  231.0 404.0 %all-gather.18.cloned.1.call-start = ((), (), s32[]{:S(2)}) async-start(), calls=%async_computation.9 | async-start | bytes 17825792 | tf_op jit(solution)/shard_map/all_gather | solution.py:87
  238.4 3.9 copy-start.50
  238.4 71.0 %copy-start.51 = (f32[128]{0:T(128)S(1)}, f32[128]{0:T(128)}, u32[]{:S(2)}) copy-start(f32[128]{0:T(128)} %param.22) | copy-start | bytes 1540
  238.4 103.8 %all-to-all-start.2 = ((bf16[16,48,2048]{2,1,0:T(8,128)(2,1)}), bf16[16,48,2048]{2,1,0:T(8,128)(2,1)S(1)}, u32[]{:S(2)}, u32[]{:S(2)}) async-start(bf16[16,48,2048]{2,1,0:T(8,128)(2,1)} %bitcast.103), calls=%async_computation.2 | async-start | bytes 6291456 | tf_op jit(solution)/shard_map/all_to_all | solution.py:79
  242.3 596.0 %all-reduce.12.cloned.1.call-start = ((), (), s32[]{:S(2)}) async-start(), calls=%async_computation.11 | async-start | bytes 12582912 | tf_op jit(solution)/shard_map/psum | solution.py:152
  309.4 325.7 %copy-start.43 = (f32[16,1,128]{2,1,0:T(1,128)}, f32[16,1,128]{2,1,0:T(1,128)S(1)}, u32[]{:S(2)}) copy-start(f32[16,1,128]{2,1,0:T(1,128)S(1)} %convert_element_type.162) | copy-start | bytes 24580
  383.2 3.2 copy-start.5
  383.2 124.7 %copy-start.7 = (bf16[768,2048]{1,0:T(8,128)(2,1)S(1)}, bf16[768,2048]{1,0:T(8,128)(2,1)}, u32[]{:S(2)}) copy-start(bf16[768,2048]{1,0:T(8,128)(2,1)} %gather_fusion.5) | copy-start | bytes 9437188
  686.7 233.5 %all-gather.22.cloned.1.call-start = ((), (), s32[]{:S(2)}) async-start(), calls=%async_computation.14 | async-start | bytes 9437184 | tf_op jit(solution)/shard_map/all_gather | solution.py:131
  686.8 31.9 %copy-start.20 = (f32[8,768]{1,0:T(8,128)S(1)}, f32[8,768]{1,0:T(8,128)}, u32[]{:S(2)}) copy-start(f32[8,768]{1,0:T(8,128)} %copy-done.19) | copy-start | bytes 73732
  686.8 31.9 %copy-start.26 = (f32[8,768]{1,0:T(8,128)S(1)}, f32[8,768]{1,0:T(8,128)}, u32[]{:S(2)}) copy-start(f32[8,768]{1,0:T(8,128)} %copy-done.25) | copy-start | bytes 73732
  718.7 459.8 %all-reduce.14.cloned.1.call-start = ((), (), s32[]{:S(2)}) async-start(), calls=%async_computation.12 | async-start | bytes 12582912 | tf_op jit(solution)/shard_map/psum | solution.py:182
  927.1 6.9 copy-start.8
  934.0 3.2 copy-start.6
  934.0 3.2 copy-start.30
  934.0 5.3 copy-start.46
  946.4 8.5 copy-start.11
  946.4 8.5 copy-start.18
  967.0 13.1 copy-start.13
  1009.7 9.3 copy-start.16
  1009.7 9.3 copy-start.45
  1024.4 943.6 %reduce-scatter.2.cloned.1.call-start = ((), (), s32[]{:S(2)}) async-start(), calls=%async_computation.13 | async-start | bytes 91357184 | tf_op jit(solution)/shard_map/reduce_scatter | solution.py:193
  1024.4 4.5 copy-start.15
  1024.4 4.5 copy-start.53
  1029.0 6.2 copy-start.44
  1089.6 88.9 %copy-start.22 = (f32[16,1,128]{2,1,0:T(1,128)S(1)}, f32[16,1,128]{2,1,0:T(1,128)}, u32[]{:S(2)}) copy-start(f32[16,1,128]{2,1,0:T(1,128)} %copy-done.21) | copy-start | bytes 24580
  1089.6 88.9 %copy-start.24 = (f32[768]{0:T(1024)S(1)}, f32[768]{0:T(1024)}, u32[]{:S(2)}) copy-start(f32[768]{0:T(1024)} %copy-done.23) | copy-start | bytes 9220
  1089.6 114.5 %all-to-all-start.1 = ((bf16[16,48,2048]{2,1,0:T(8,128)(2,1)}), bf16[16,48,2048]{2,1,0:T(8,128)(2,1)S(1)}, u32[]{:S(2)}, u32[]{:S(2)}) async-start(bf16[16,48,2048]{2,1,0:T(8,128)(2,1)} %bitcast.102), calls=%async_computation.1 | async-start | bytes 6291456 | tf_op jit(solution)/shard_map/all_to_all | solution.py:222
  1095.4 89.3 %copy-start.28 = (f32[768]{0:T(1024)S(1)}, f32[768]{0:T(1024)}, u32[]{:S(2)}) copy-start(f32[768]{0:T(1024)} %copy-done.27) | copy-start | bytes 9220
  1178.5 6.1 copy-start.33
  1178.5 6.2 copy-start.3
  1184.6 3.0 copy-start.9
  1184.6 3.0 copy-start.31
  1187.7 6.3 copy-start.35
  1204.1 6.2 copy-start.40
  1204.1 10.6 copy-start.54
  1204.1 119.4 %all-to-all-start.3 = ((bf16[16,48,2048]{2,1,0:T(8,128)(2,1)}), bf16[16,48,2048]{2,1,0:T(8,128)(2,1)}, u32[]{:S(2)}, u32[]{:S(2)}) async-start(bf16[16,48,2048]{2,1,0:T(8,128)(2,1)} %bitcast.101), calls=%async_computation.3 | async-start | bytes 6291456 | tf_op jit(solution)/shard_map/all_to_all | solution.py:223
  1215.9 4.3 copy-start.36
  1216.0 4.3 copy-start.37
  1216.0 4.3 copy-start.38
  1323.4 653.0 %copy-start.1 = (bf16[768,2048]{1,0:T(8,128)(2,1)S(1)}, bf16[768,2048]{1,0:T(8,128)(2,1)}, u32[]{:S(2)}) copy-start(bf16[768,2048]{1,0:T(8,128)(2,1)} %param.13) | copy-start | bytes 9437188
  (5 other events, 4.1 us)
Sparse Core Ops, SparseCore 0:
  10.7 62.2 all-gather.11
  75.7 56.6 all-gather.13
  134.6 50.0 all-gather.15
  228.2 150.4 all-reduce.9
  381.3 126.4 all-gather.19
  510.4 124.5 all-gather.17
  686.9 151.4 all-reduce.11
  839.9 80.3 all-gather.21
  1024.5 153.9 all-reduce.13
  1182.6 785.3 reduce-scatter.1
